TPU v7x, 32 devices: a whole 2x2x4 slice. The times are simulated.
32 devices in a mesh: seq: 2 (over x), head: 4 (over z), dp: 4 (over y, core).
Axes of the slice: x: 2, y: 2, z: 4, core: 2. Of those that a mesh axis runs over, the one named last changes fastest.
Arguments:
- queries: bfloat16 [4, 512, 64, 128], P('dp', 'seq', 'head'), may hold values from -6 to 6
- keys: bfloat16 [4, 512, 8, 128], P('dp', 'seq', 'head'), may hold values from -6 to 6
- values: bfloat16 [4, 512, 8, 128], P('dp', 'seq', 'head'), may hold values from -6 to 6
- attn_out: bfloat16 [4, 512, 64, 128], P('dp', 'seq', 'head'), may hold values from -6 to 6
- out_grad: bfloat16 [4, 512, 64, 128], P('dp', 'seq', 'head'), may hold values from -6 to 6
- gate_values: float32 [4, 64, 512], P('dp', 'head', 'seq'), may hold values from 0.05 to 0.95
- log_totals: float32 [4, 64, 512], P('dp', 'head', 'seq'), may hold values from 3 to 5
- hidden: bfloat16 [4, 512, 5120], P('dp', 'seq', 'head'), may hold values from -6 to 6
- block_ids: int32 [4, 8, 8, 16], P('dp', 'seq', 'head'), may hold values from 0 to 7, as said below
- block_valid: int32 [4, 8, 8, 16], P('dp', 'seq', 'head'), may hold values from 0 to 1
Outputs:
- query_grad: bfloat16 [4, 512, 64, 128], P('dp', 'seq', 'head')
- key_grad: bfloat16 [4, 512, 8, 128], P('dp', 'seq', 'head')
- value_grad: bfloat16 [4, 512, 8, 128], P('dp', 'seq', 'head')
- gate_weight_grad: float32 [64, 5120], P(None, 'head')
Inputs may be any that keep to these rules, and one draw needn't show every extreme that they name: `block_ids`: for query tile t and key head k, the slots whose block_valid is 1 name distinct blocks of index at most t, among them block t itself and block 0; exactly min(16, t + 1) slots are valid. The ids of the other slots are any blocks, and may repeat a valid one.
All inputs are finite; a program needn't handle non-finite values.
Results may differ from a plain program's by a relative error of at most 0.025.
Values may be sent and summed in bfloat16 or wider, within the bound.
A program may use at most 128 MiB of HBM per device.

v0:
```python
import math
import jax
import jax.numpy as jnp
from jax import lax
from jax.sharding import PartitionSpec as P


def on_device(
    queries,
    keys,
    values,
    attn_out,
    out_grad,
    gate_values,
    log_totals,
    hidden,
    block_ids,
    block_valid,
):
    tokens_here = queries.shape[1]
    heads_here = queries.shape[2]
    kv_heads = keys.shape[2]
    head_width = queries.shape[3]
    group_size = heads_here // kv_heads
    tiles_here = block_ids.shape[1]
    block_rows = tokens_here // tiles_here
    seq_count = lax.axis_size("seq")
    all_blocks = tiles_here * seq_count
    factor = head_width ** (-0.5)
    chosen = block_ids[0]
    usable = block_valid[0] > 0
    head_rows = jnp.arange(kv_heads, dtype=jnp.int32)[None, :, None]
    offsets = jnp.arange(block_rows, dtype=jnp.int32)
    whole_keys, whole_values = (
        lax.all_gather(keys, "seq", axis=1, tiled=True),
        lax.all_gather(values, "seq", axis=1, tiled=True),
    )
    key_sel = whole_keys[0].reshape(all_blocks, block_rows, kv_heads, head_width)[
        chosen, :, head_rows, :
    ]
    value_sel = whole_values[0].reshape(all_blocks, block_rows, kv_heads, head_width)[
        chosen, :, head_rows, :
    ]
    query_tiles = queries[0].reshape(tiles_here, block_rows, kv_heads, group_size, head_width)
    output_tiles = attn_out[0].reshape(tiles_here, block_rows, kv_heads, group_size, head_width)
    upstream_tiles = out_grad[0].reshape(tiles_here, block_rows, kv_heads, group_size, head_width)
    gate_tiles = jnp.transpose(
        gate_values[0].reshape(kv_heads, group_size, tiles_here, block_rows), (2, 0, 1, 3)
    )
    total_tiles = jnp.transpose(
        log_totals[0].reshape(kv_heads, group_size, tiles_here, block_rows), (2, 0, 1, 3)
    )
    tile_numbers = lax.axis_index("seq") * tiles_here + jnp.arange(tiles_here, dtype=jnp.int32)

    def tile_math(tile_items):
        (
            tile_number,
            query_tile,
            output_tile,
            upstream,
            gate_tile,
            totals,
            picked,
            usable_tile,
            key_tile,
            value_tile,
        ) = tile_items
        gates_by_row = jnp.transpose(gate_tile, (2, 0, 1))
        grad_output = (gates_by_row[..., None] * upstream.astype(jnp.float32)).astype(jnp.bfloat16)
        output_wide = output_tile.astype(jnp.float32)
        row_delta = jnp.transpose(
            jnp.sum(grad_output.astype(jnp.float32) * output_wide, axis=-1), (1, 2, 0)
        )
        gate_grad = jnp.sum(upstream.astype(jnp.float32) * output_wide, axis=-1)
        logit_grad = (gate_grad * gates_by_row * (1.0 - gates_by_row)).astype(jnp.bfloat16)
        scores = (
            jnp.einsum("ikgd,knjd->kginj", query_tile, key_tile, preferred_element_type=jnp.float32)
            * factor
        )
        query_pos = tile_number * block_rows + offsets
        key_pos = picked[..., None] * block_rows + offsets
        allowed = usable_tile[:, None, :, None] & (
            key_pos[:, None, :, :] <= query_pos[None, :, None, None]
        )
        probability = jnp.where(allowed[:, None], jnp.exp(scores - totals[..., None, None]), 0.0)
        prob_grad = jnp.einsum(
            "ikgd,knjd->kginj", grad_output, value_tile, preferred_element_type=jnp.float32
        )
        dscore = (probability * (prob_grad - row_delta[..., None, None])).astype(jnp.bfloat16)
        prob_low = probability.astype(jnp.bfloat16)
        query_part = (
            jnp.einsum("kginj,knjd->ikgd", dscore, key_tile, preferred_element_type=jnp.float32)
            * factor
        ).astype(jnp.bfloat16)
        key_part = (
            jnp.einsum("kginj,ikgd->knjd", dscore, query_tile, preferred_element_type=jnp.float32)
            * factor
        )
        value_part = jnp.einsum(
            "kginj,ikgd->knjd", prob_low, grad_output, preferred_element_type=jnp.float32
        )
        return (query_part, logit_grad, jnp.concatenate([key_part, value_part], axis=-1))

    def tile_step(partial_value, tile_items):
        query_part, logit_grad, paired = tile_math(tile_items)
        return (partial_value, (query_part, logit_grad, paired))

    tile_items = (
        tile_numbers,
        query_tiles,
        output_tiles,
        upstream_tiles,
        gate_tiles,
        total_tiles,
        chosen,
        usable,
        key_sel,
        value_sel,
    )
    unused, (query_parts, logit_parts, paired_all) = lax.scan(
        tile_step, jnp.zeros((), jnp.float32), tile_items
    )
    span_blocks = tokens_here * lax.axis_size("seq") // block_rows
    target = chosen
    target = jnp.where((target >= 0) & (target < span_blocks), target, span_blocks)
    holder = jnp.zeros((span_blocks, block_rows, kv_heads, 2 * head_width), jnp.float32)
    holder = holder.at[target, :, head_rows, :].add(paired_all, mode="drop")
    summed = lax.psum_scatter(
        holder.reshape(tokens_here * lax.axis_size("seq"), kv_heads, 2 * head_width).astype(
            jnp.bfloat16
        ),
        "seq",
        scatter_dimension=0,
        tiled=True,
    ).astype(jnp.float32)
    query_grad = query_parts.reshape(1, tokens_here, heads_here, head_width)
    logit_rows = jnp.transpose(logit_parts.reshape(tokens_here, heads_here))[None]
    every_logit = lax.all_gather(logit_rows, "head", axis=1, tiled=True)
    weight_part = jnp.dot(every_logit[0], hidden[0], preferred_element_type=jnp.float32)
    weight_scale = 1.0 / math.sqrt(lax.axis_size("dp") * seq_count * tokens_here)
    gate_weight_grad = lax.psum(weight_part, ("seq", "dp")) * weight_scale
    key_grad = summed[None, :, :, :head_width].astype(jnp.bfloat16)
    value_grad = summed[None, :, :, head_width:].astype(jnp.bfloat16)
    return (query_grad, key_grad, value_grad, gate_weight_grad)


def solution(mesh):
    return jax.shard_map(
        on_device,
        mesh=mesh,
        in_specs=(
            P("dp", "seq", "head", None),
            P("dp", "seq", "head", None),
            P("dp", "seq", "head", None),
            P("dp", "seq", "head", None),
            P("dp", "seq", "head", None),
            P("dp", "head", "seq"),
            P("dp", "head", "seq"),
            P("dp", "seq", "head"),
            P("dp", "seq", "head", None),
            P("dp", "seq", "head", None),
        ),
        out_specs=(
            P("dp", "seq", "head", None),
            P("dp", "seq", "head", None),
            P("dp", "seq", "head", None),
            P(None, "head"),
        ),
        check_vma=False,
    )
```

profile of v0, /device:TPU:0, one launch (start us, length us, event | category | flops | bytes accessed | tf_op | source)
XLA Modules:
  0.0 180.2 jit_solution(4722716227157090044)
XLA Ops:
  8.1 0.9 copy.32
  9.0 7.1 %all_gather.9 = bf16[1,512,2,128]{3,1,2,0:T(8,128)(2,1)S(1)} all-gather(bf16[1,256,2,128]{3,1,2,0:T(8,128)(2,1)S(1)} %copy.32), channel_id=1, replica_groups=mesh['seq'=2,'head'=4,'dp'=4] {'seq'}, dimensions={1}, use_global_device_ids=true | all-gather | bytes 393216 | tf_op jit(solution)/shard_map/all_gather | solution.py:35
  16.2 0.7 or_select_fusion
  17.0 0.7 compare_bitcast_fusion
  17.7 0.8 reshape_squeeze.23
  18.5 0.9 copy.35
  19.4 5.6 %all_gather.10 = bf16[1,512,2,128]{3,1,2,0:T(8,128)(2,1)S(1)} all-gather(bf16[1,256,2,128]{3,1,2,0:T(8,128)(2,1)S(1)} %copy.35), channel_id=1, replica_groups=mesh['seq'=2,'head'=4,'dp'=4] {'seq'}, dimensions={1}, use_global_device_ids=true | all-gather | bytes 393216 | tf_op jit(solution)/shard_map/all_gather | solution.py:36
  25.1 1.1 gather_fusion
  26.1 2.3 %gather_fusion.1 = bf16[128,64,128]{2,1,0:T(8,128)(2,1)} fusion(bf16[8,64,2,128]{3,1,2,0:T(8,128)(2,1)S(1)} %copy.36, s32[128]{0:T(128)S(1)} %reshape.124), kind=kCustom, calls=%fused_computation.1 | custom fusion | bytes 4195328 | tf_op jit(solution)/shard_map/gather | solution.py:41
  28.6 69.9 %while.16 = (s32[]{:T(128)}, bf16[4,64,2,8,128]{4,3,2,1,0:T(8,128)(2,1)}, bf16[4,64,2,8]{1,3,2,0:T(8,128)(2,1)S(1)}, f32[4,2,16,64,256]{4,3,2,1,0:T(8,128)}, bf1...) while((s32[]{:T(128)}, ...), condition=%wide.region_3.4_spmd.clone.clone, body=%wide.region_0.3_spmd.clone.clone.sunk | while | flops 1355944064 | bytes 33248452 | solution.py:120
  28.6 1.0 constant_dynamic-slice_fusion.10
  29.6 1.3 fusion.78
  30.8 1.1 constant_dynamic-slice_fusion.11
  31.9 0.5 fusion.79
  32.5 0.6 dynamic_slice.98
  33.7 0.7 fusion.80
  35.0 4.0 %fusion.82 = bf16[2,8,64,16,64]{2,4,1,3,0:T(8,128)(2,1)S(1)} fusion(f32[2,16,64,64,8]{3,2,4,1,0:T(8,128)S(1)} %fusion.78, f32[2,8,64]{2,1,0:T(8,128)S(1)} %bitcast.222, f32[2,8,64]{2,1,0:T(8,128)S(1)} %bitcast.223, pred[2,64,16,64]{1,3,2,0:T(8,128)(4,1)S(1)} %compare_and_fusion.2, bf16[4,2,16,64,128]{4,3,2,1,0:T(8,128)(2,1)} %get-tuple-element.380, ...), kind=kOutput, calls=%fused_computation.6.clone.1 | convolution fusion | flops 275120128 | bytes 7221252 | tf_op jit(solution)/shard_map/while/body/eval_jaxpr/ikgd,knjd->kginj/dot_general | solution.py:86
  39.0 1.3 fusion.83
  40.3 0.9 copy_dynamic-update-slice_fusion.2
  41.2 2.4 %fusion.85 = f32[2,16,64,128]{3,2,1,0:T(8,128)S(1)} fusion(f32[2,16,64,64,8]{3,2,4,1,0:T(8,128)S(1)} %fusion.78, f32[2,8,64]{2,1,0:T(8,128)S(1)} %bitcast.224, pred[2,64,16,64]{1,3,2,0:T(8,128)(4,1)S(1)} %compare_and_fusion.2, f32[64,2,8]{0,2,1:T(8,128)S(1)} %bitcast.216, bf16[1,64,2,8,128]{4,3,2,1,0:T(8,128)(2,1)S(1)} %get-tuple-element.332), kind=kOutput, calls=%fused_computation.17.clone.1 | convolution fusion | flops 273022976 | bytes 5644288 | tf_op jit(solution)/shard_map/while/body/eval_jaxpr/kginj,ikgd->knjd/dot_general | solution.py:99
  43.6 0.9 fusion.86
  44.6 1.5 fusion.87
  46.1 1.0 constant_dynamic-slice_fusion.10
  47.0 1.3 fusion.78
  48.3 1.1 constant_dynamic-slice_fusion.11
  49.9 0.6 dynamic_slice.98
  51.2 0.7 fusion.80
  52.4 4.0 %fusion.82 = bf16[2,8,64,16,64]{2,4,1,3,0:T(8,128)(2,1)S(1)} fusion(f32[2,16,64,64,8]{3,2,4,1,0:T(8,128)S(1)} %fusion.78, f32[2,8,64]{2,1,0:T(8,128)S(1)} %bitcast.222, f32[2,8,64]{2,1,0:T(8,128)S(1)} %bitcast.223, pred[2,64,16,64]{1,3,2,0:T(8,128)(4,1)S(1)} %compare_and_fusion.2, bf16[4,2,16,64,128]{4,3,2,1,0:T(8,128)(2,1)} %get-tuple-element.380, ...), kind=kOutput, calls=%fused_computation.6.clone.1 | convolution fusion | flops 275120128 | bytes 7221252 | tf_op jit(solution)/shard_map/while/body/eval_jaxpr/ikgd,knjd->kginj/dot_general | solution.py:86
  56.5 1.3 fusion.83
  57.8 0.9 copy_dynamic-update-slice_fusion.2
  58.7 2.4 %fusion.85 = f32[2,16,64,128]{3,2,1,0:T(8,128)S(1)} fusion(f32[2,16,64,64,8]{3,2,4,1,0:T(8,128)S(1)} %fusion.78, f32[2,8,64]{2,1,0:T(8,128)S(1)} %bitcast.224, pred[2,64,16,64]{1,3,2,0:T(8,128)(4,1)S(1)} %compare_and_fusion.2, f32[64,2,8]{0,2,1:T(8,128)S(1)} %bitcast.216, bf16[1,64,2,8,128]{4,3,2,1,0:T(8,128)(2,1)S(1)} %get-tuple-element.332), kind=kOutput, calls=%fused_computation.17.clone.1 | convolution fusion | flops 273022976 | bytes 5644288 | tf_op jit(solution)/shard_map/while/body/eval_jaxpr/kginj,ikgd->knjd/dot_general | solution.py:99
  61.1 0.9 fusion.86
  62.1 1.4 fusion.87
  63.5 1.0 constant_dynamic-slice_fusion.10
  64.5 1.3 fusion.78
  65.7 1.1 constant_dynamic-slice_fusion.11
  67.4 0.6 dynamic_slice.98
  68.6 0.7 fusion.80
  69.9 4.0 %fusion.82 = bf16[2,8,64,16,64]{2,4,1,3,0:T(8,128)(2,1)S(1)} fusion(f32[2,16,64,64,8]{3,2,4,1,0:T(8,128)S(1)} %fusion.78, f32[2,8,64]{2,1,0:T(8,128)S(1)} %bitcast.222, f32[2,8,64]{2,1,0:T(8,128)S(1)} %bitcast.223, pred[2,64,16,64]{1,3,2,0:T(8,128)(4,1)S(1)} %compare_and_fusion.2, bf16[4,2,16,64,128]{4,3,2,1,0:T(8,128)(2,1)} %get-tuple-element.380, ...), kind=kOutput, calls=%fused_computation.6.clone.1 | convolution fusion | flops 275120128 | bytes 7221252 | tf_op jit(solution)/shard_map/while/body/eval_jaxpr/ikgd,knjd->kginj/dot_general | solution.py:86
  73.9 1.3 fusion.83
  75.2 0.9 copy_dynamic-update-slice_fusion.2
  76.1 2.4 %fusion.85 = f32[2,16,64,128]{3,2,1,0:T(8,128)S(1)} fusion(f32[2,16,64,64,8]{3,2,4,1,0:T(8,128)S(1)} %fusion.78, f32[2,8,64]{2,1,0:T(8,128)S(1)} %bitcast.224, pred[2,64,16,64]{1,3,2,0:T(8,128)(4,1)S(1)} %compare_and_fusion.2, f32[64,2,8]{0,2,1:T(8,128)S(1)} %bitcast.216, bf16[1,64,2,8,128]{4,3,2,1,0:T(8,128)(2,1)S(1)} %get-tuple-element.332), kind=kOutput, calls=%fused_computation.17.clone.1 | convolution fusion | flops 273022976 | bytes 5644288 | tf_op jit(solution)/shard_map/while/body/eval_jaxpr/kginj,ikgd->knjd/dot_general | solution.py:99
  78.5 0.9 fusion.86
  79.5 1.5 fusion.87
  81.0 1.0 constant_dynamic-slice_fusion.10
  81.9 1.3 fusion.78
  83.2 1.1 constant_dynamic-slice_fusion.11
  84.8 0.6 dynamic_slice.98
  86.1 0.7 fusion.80
  87.3 4.0 %fusion.82 = bf16[2,8,64,16,64]{2,4,1,3,0:T(8,128)(2,1)S(1)} fusion(f32[2,16,64,64,8]{3,2,4,1,0:T(8,128)S(1)} %fusion.78, f32[2,8,64]{2,1,0:T(8,128)S(1)} %bitcast.222, f32[2,8,64]{2,1,0:T(8,128)S(1)} %bitcast.223, pred[2,64,16,64]{1,3,2,0:T(8,128)(4,1)S(1)} %compare_and_fusion.2, bf16[4,2,16,64,128]{4,3,2,1,0:T(8,128)(2,1)} %get-tuple-element.380, ...), kind=kOutput, calls=%fused_computation.6.clone.1 | convolution fusion | flops 275120128 | bytes 7221252 | tf_op jit(solution)/shard_map/while/body/eval_jaxpr/ikgd,knjd->kginj/dot_general | solution.py:86
  91.4 1.3 fusion.83
  92.7 0.9 copy_dynamic-update-slice_fusion.2
  93.6 2.4 %fusion.85 = f32[2,16,64,128]{3,2,1,0:T(8,128)S(1)} fusion(f32[2,16,64,64,8]{3,2,4,1,0:T(8,128)S(1)} %fusion.78, f32[2,8,64]{2,1,0:T(8,128)S(1)} %bitcast.224, pred[2,64,16,64]{1,3,2,0:T(8,128)(4,1)S(1)} %compare_and_fusion.2, f32[64,2,8]{0,2,1:T(8,128)S(1)} %bitcast.216, bf16[1,64,2,8,128]{4,3,2,1,0:T(8,128)(2,1)S(1)} %get-tuple-element.332), kind=kOutput, calls=%fused_computation.17.clone.1 | convolution fusion | flops 273022976 | bytes 5644288 | tf_op jit(solution)/shard_map/while/body/eval_jaxpr/kginj,ikgd->knjd/dot_general | solution.py:99
  96.0 0.9 fusion.86
  96.9 1.5 fusion.87
  98.5 13.6 %all-gather = bf16[64,256]{1,0:T(8,128)(2,1)S(1)} all-gather(bf16[16,256]{1,0:T(8,128)(2,1)S(1)} %bitcast.227), channel_id=2, replica_groups=mesh['seq'=2,'head'=4,'dp'=4] {'head'}, dimensions={0}, use_global_device_ids=true | all-gather | bytes 40960 | tf_op jit(solution)/shard_map/all_gather | solution.py:138
  112.2 1.0 fusion.42
  113.4 19.1 %scatter_fusion = f32[8,64,2,256]{3,1,2,0:T(8,128)S(1)} fusion(f32[8,64,2,256]{3,1,2,0:T(8,128)S(1)} %broadcast_in_dim.53, s32[128]{0:T(128)S(1)} %reshape.136, f32[128,64,256]{2,1,0:T(8,128)} %bitcast.210), kind=kCustom, calls=%fused_computation.2 | custom fusion | flops 2097152 | bytes 25166848 | tf_op jit(solution)/shard_map/scatter-add | solution.py:127
  132.5 0.8 copy.44
  133.4 35.1 %all-reduce.2.cloned.1.call-done = f32[64,1280]{1,0:T(8,128)} async-done(((f32[64,1280]{1,0:T(8,128)}), f32[64,1280]{1,0:T(8,128)}) %all-reduce.2.cloned.1.call-update) | async-done | bytes 327696 | tf_op jit(solution)/shard_map/psum | solution.py:141
  168.5 1.7 broadcast_multiply_fusion
  170.2 1.0 slice_bitcast_fusion
  171.2 0.8 copy.46
  172.0 0.8 copy.47
  (49 shorter events, 4.6 us)
Async XLA Ops:
  8.0 104.2 %copy-start = (bf16[1,256,1280]{2,1,0:T(8,128)(2,1)S(1)}, bf16[1,256,1280]{2,1,0:T(8,128)(2,1)}, u32[]{:S(2)}) copy-start(bf16[1,256,1280]{2,1,0:T(8,128)(2,1)} %param.19) | copy-start | bytes 1966084
  8.0 20.5 %copy-start.1 = (f32[1,16,256]{2,1,0:T(8,128)S(1)}, f32[1,16,256]{2,1,0:T(8,128)}, u32[]{:S(2)}) copy-start(f32[1,16,256]{2,1,0:T(8,128)} %param.17) | copy-start | bytes 49156
  8.0 160.4 %all-reduce.2.cloned.1.call-start = ((), (), s32[]{:S(2)}) async-start(), calls=%async_computation.2 | async-start | bytes 655360 | tf_op jit(solution)/shard_map/psum | solution.py:141
  113.2 57.0 %reduce-scatter.2.cloned.1.call-start = ((), (), s32[]{:S(2)}) async-start(), calls=%async_computation.1 | async-start | bytes 786432 | tf_op jit(solution)/shard_map/reduce_scatter | solution.py:128
Sparse Core Ops, SparseCore 0:
  113.3 55.1 all-reduce.1
Sparse Core Ops, SparseCore 1:
  133.5 15.6 reduce-scatter.1
where the time goes:
time: 181 us; the launch traced here: 180 us
  matrix products  40.9 us (23%)
  other arithmetic  35.2 us (19%)
  waiting for transfers between devices  35.1 us (19%)
  blocking collectives  26.4 us (15%)
  local copies, waits for them, and re-layouts  24.1 us (13%)
  between operations  15.6 us (9%)
  loops' own time  2.88 us (2%)
    psum x1, waiting for transfers between devices, on_device(): gate_weight_grad = lax.psum(weight_part, ('seq', 'dp')) * weight_scale  35.1 us
    scatter-add x1, other arithmetic, on_device(): holder = holder.at[target, :, head_rows, :].add(paired_all, mode='drop')  19.1 us
    dot_general x4, matrix products, tile_math(): jnp.einsum('ikgd,knjd->kginj', grad_output, value_tile, preferred_element...  16.1 us
    all_gather x1, blocking collectives, on_device(): every_logit = lax.all_gather(logit_rows, 'head', axis=1, tiled=True)  13.6 us
    dynamic_slice x16, local copies, waits for them, and re-layouts, on_device(): lax.scan(tile_step, jnp.zeros((), jnp.float32), tile_items)  10.6 us
    dot_general x4, matrix products, tile_math(): jnp.einsum('kginj,ikgd->knjd', prob_low, grad_output, preferred_element_t...  9.55 us
    all_gather x1, blocking collectives, on_device(): lax.all_gather(keys, 'seq', axis=1, tiled=True)  7.12 us
    dynamic_update_slice x8, other arithmetic, on_device(): lax.scan(tile_step, jnp.zeros((), jnp.float32), tile_items)  5.93 us
  transfers between devices with their start and end apart: 2, of which 1 were waited for; matrix products, arithmetic and copies ran while one was open for 12% of the time, Pallas kernels for 0%

commit v1 on v0

--- a/solution.py
+++ b/solution.py
@@ -138,7 +138,7 @@
     every_logit = lax.all_gather(logit_rows, "head", axis=1, tiled=True)
     weight_part = jnp.dot(every_logit[0], hidden[0], preferred_element_type=jnp.float32)
     weight_scale = 1.0 / math.sqrt(lax.axis_size("dp") * seq_count * tokens_here)
-    gate_weight_grad = lax.psum(weight_part, ("seq", "dp")) * weight_scale
+    gate_weight_grad = jnp.sum(lax.all_gather(weight_part, ("seq", "dp")), axis=0) * weight_scale
     key_grad = summed[None, :, :, :head_width].astype(jnp.bfloat16)
     value_grad = summed[None, :, :, head_width:].astype(jnp.bfloat16)
     return (query_grad, key_grad, value_grad, gate_weight_grad)

time: 181 us -> 176 us (0.972)
  waiting for transfers between devices: 35.1 us -> 28.5 us
    psum x1 -> x0, waiting for transfers between devices: 35.1 us -> none  [on_device(): gate_weight_grad = lax.psum(weight_part, ('seq', 'dp')) * weight_scale]
    all_gather x0 -> x1, waiting for transfers between devices: none -> 26.9 us  [on_device(): lax.all_gather(weight_part, ('seq', 'dp'))]
    reduce_sum x0 -> x1, other arithmetic: none -> 1.9 us  [on_device(): jnp.sum(lax.all_gather(weight_part, ('seq', 'dp')), axis=0) * weight_scale]
  transfers between devices with their start and end apart: 2 -> 2, of which waited for: 1 -> 2; matrix products, arithmetic and copies ran while one was open for 12% -> 2% of each run, Pallas kernels for 0% -> 0%
where the time goes in v1:
time: 176 us; the launch traced here: 174 us
  matrix products  40.9 us (23%)
  other arithmetic  36.1 us (21%)
  waiting for transfers between devices  28.5 us (16%)
  blocking collectives  26.4 us (15%)
  local copies, waits for them, and re-layouts  24.1 us (14%)
  between operations  15.6 us (9%)
  loops' own time  2.88 us (2%)
    all_gather x1, waiting for transfers between devices, on_device(): lax.all_gather(weight_part, ('seq', 'dp'))  26.9 us
    scatter-add x1, other arithmetic, on_device(): holder = holder.at[target, :, head_rows, :].add(paired_all, mode='drop')  19 us
    dot_general x4, matrix products, tile_math(): jnp.einsum('ikgd,knjd->kginj', grad_output, value_tile, preferred_element...  16.1 us
    all_gather x1, blocking collectives, on_device(): every_logit = lax.all_gather(logit_rows, 'head', axis=1, tiled=True)  13.6 us
    dynamic_slice x16, local copies, waits for them, and re-layouts, on_device(): lax.scan(tile_step, jnp.zeros((), jnp.float32), tile_items)  10.6 us
    dot_general x4, matrix products, tile_math(): jnp.einsum('kginj,ikgd->knjd', prob_low, grad_output, preferred_element_t...  9.55 us
    all_gather x1, blocking collectives, on_device(): lax.all_gather(keys, 'seq', axis=1, tiled=True)  7.12 us
    dynamic_update_slice x8, other arithmetic, on_device(): lax.scan(tile_step, jnp.zeros((), jnp.float32), tile_items)  5.93 us
  transfers between devices with their start and end apart: 2, of which 2 were waited for; matrix products, arithmetic and copies ran while one was open for 2% of the time, Pallas kernels for 0%

profile of v1, /device:TPU:0, one launch (start us, length us, event | category | flops | bytes accessed | tf_op | source)
XLA Modules:
  0.0 174.5 jit_solution(846792042026959762)
XLA Ops:
  8.1 0.9 copy.32
  9.0 7.1 %all_gather.15 = bf16[1,512,2,128]{3,1,2,0:T(8,128)(2,1)S(1)} all-gather(bf16[1,256,2,128]{3,1,2,0:T(8,128)(2,1)S(1)} %copy.32), channel_id=1, replica_groups=mesh['seq'=2,'head'=4,'dp'=4] {'seq'}, dimensions={1}, use_global_device_ids=true | all-gather | bytes 393216 | tf_op jit(solution)/shard_map/all_gather | solution.py:35
  16.2 0.7 or_select_fusion
  17.0 0.7 compare_bitcast_fusion
  17.7 0.8 reshape_squeeze.23
  18.5 0.9 copy.35
  19.4 5.6 %all_gather.16 = bf16[1,512,2,128]{3,1,2,0:T(8,128)(2,1)S(1)} all-gather(bf16[1,256,2,128]{3,1,2,0:T(8,128)(2,1)S(1)} %copy.35), channel_id=1, replica_groups=mesh['seq'=2,'head'=4,'dp'=4] {'seq'}, dimensions={1}, use_global_device_ids=true | all-gather | bytes 393216 | tf_op jit(solution)/shard_map/all_gather | solution.py:36
  25.1 1.1 gather_fusion
  26.1 2.3 %gather_fusion.1 = bf16[128,64,128]{2,1,0:T(8,128)(2,1)} fusion(bf16[8,64,2,128]{3,1,2,0:T(8,128)(2,1)S(1)} %copy.36, s32[128]{0:T(128)S(1)} %reshape.124), kind=kCustom, calls=%fused_computation.1 | custom fusion | bytes 4195328 | tf_op jit(solution)/shard_map/gather | solution.py:41
  28.6 69.9 %while.16 = (s32[]{:T(128)}, bf16[4,64,2,8,128]{4,3,2,1,0:T(8,128)(2,1)}, bf16[4,64,2,8]{1,3,2,0:T(8,128)(2,1)S(1)}, f32[4,2,16,64,256]{4,3,2,1,0:T(8,128)}, bf1...) while((s32[]{:T(128)}, ...), condition=%wide.region_3.4_spmd.clone.clone, body=%wide.region_0.3_spmd.clone.clone.sunk | while | flops 1355944064 | bytes 33248452 | solution.py:120
  28.6 1.0 constant_dynamic-slice_fusion.10
  29.6 1.3 fusion.78
  30.8 1.1 constant_dynamic-slice_fusion.11
  32.5 0.6 dynamic_slice.98
  33.7 0.7 fusion.80
  35.0 4.0 %fusion.82 = bf16[2,8,64,16,64]{2,4,1,3,0:T(8,128)(2,1)S(1)} fusion(f32[2,16,64,64,8]{3,2,4,1,0:T(8,128)S(1)} %fusion.78, f32[2,8,64]{2,1,0:T(8,128)S(1)} %bitcast.224, f32[2,8,64]{2,1,0:T(8,128)S(1)} %bitcast.225, pred[2,64,16,64]{1,3,2,0:T(8,128)(4,1)S(1)} %compare_and_fusion.2, bf16[4,2,16,64,128]{4,3,2,1,0:T(8,128)(2,1)} %get-tuple-element.380, ...), kind=kOutput, calls=%fused_computation.6.clone.1 | convolution fusion | flops 275120128 | bytes 7221252 | tf_op jit(solution)/shard_map/while/body/eval_jaxpr/ikgd,knjd->kginj/dot_general | solution.py:86
  39.0 1.3 fusion.83
  40.3 0.9 copy_dynamic-update-slice_fusion.2
  41.2 2.4 %fusion.85 = f32[2,16,64,128]{3,2,1,0:T(8,128)S(1)} fusion(f32[2,16,64,64,8]{3,2,4,1,0:T(8,128)S(1)} %fusion.78, f32[2,8,64]{2,1,0:T(8,128)S(1)} %bitcast.226, pred[2,64,16,64]{1,3,2,0:T(8,128)(4,1)S(1)} %compare_and_fusion.2, f32[64,2,8]{0,2,1:T(8,128)S(1)} %bitcast.218, bf16[1,64,2,8,128]{4,3,2,1,0:T(8,128)(2,1)S(1)} %get-tuple-element.332), kind=kOutput, calls=%fused_computation.17.clone.1 | convolution fusion | flops 273022976 | bytes 5644288 | tf_op jit(solution)/shard_map/while/body/eval_jaxpr/kginj,ikgd->knjd/dot_general | solution.py:99
  43.6 0.9 fusion.86
  44.6 1.5 fusion.87
  46.1 1.0 constant_dynamic-slice_fusion.10
  47.0 1.3 fusion.78
  48.3 1.1 constant_dynamic-slice_fusion.11
  49.9 0.6 dynamic_slice.98
  51.2 0.7 fusion.80
  52.4 4.0 %fusion.82 = bf16[2,8,64,16,64]{2,4,1,3,0:T(8,128)(2,1)S(1)} fusion(f32[2,16,64,64,8]{3,2,4,1,0:T(8,128)S(1)} %fusion.78, f32[2,8,64]{2,1,0:T(8,128)S(1)} %bitcast.224, f32[2,8,64]{2,1,0:T(8,128)S(1)} %bitcast.225, pred[2,64,16,64]{1,3,2,0:T(8,128)(4,1)S(1)} %compare_and_fusion.2, bf16[4,2,16,64,128]{4,3,2,1,0:T(8,128)(2,1)} %get-tuple-element.380, ...), kind=kOutput, calls=%fused_computation.6.clone.1 | convolution fusion | flops 275120128 | bytes 7221252 | tf_op jit(solution)/shard_map/while/body/eval_jaxpr/ikgd,knjd->kginj/dot_general | solution.py:86
  56.5 1.3 fusion.83
  57.8 0.9 copy_dynamic-update-slice_fusion.2
  58.7 2.4 %fusion.85 = f32[2,16,64,128]{3,2,1,0:T(8,128)S(1)} fusion(f32[2,16,64,64,8]{3,2,4,1,0:T(8,128)S(1)} %fusion.78, f32[2,8,64]{2,1,0:T(8,128)S(1)} %bitcast.226, pred[2,64,16,64]{1,3,2,0:T(8,128)(4,1)S(1)} %compare_and_fusion.2, f32[64,2,8]{0,2,1:T(8,128)S(1)} %bitcast.218, bf16[1,64,2,8,128]{4,3,2,1,0:T(8,128)(2,1)S(1)} %get-tuple-element.332), kind=kOutput, calls=%fused_computation.17.clone.1 | convolution fusion | flops 273022976 | bytes 5644288 | tf_op jit(solution)/shard_map/while/body/eval_jaxpr/kginj,ikgd->knjd/dot_general | solution.py:99
  61.1 0.9 fusion.86
  62.1 1.4 fusion.87
  63.5 1.0 constant_dynamic-slice_fusion.10
  64.5 1.3 fusion.78
  65.7 1.1 constant_dynamic-slice_fusion.11
  67.4 0.6 dynamic_slice.98
  68.6 0.7 fusion.80
  69.9 4.0 %fusion.82 = bf16[2,8,64,16,64]{2,4,1,3,0:T(8,128)(2,1)S(1)} fusion(f32[2,16,64,64,8]{3,2,4,1,0:T(8,128)S(1)} %fusion.78, f32[2,8,64]{2,1,0:T(8,128)S(1)} %bitcast.224, f32[2,8,64]{2,1,0:T(8,128)S(1)} %bitcast.225, pred[2,64,16,64]{1,3,2,0:T(8,128)(4,1)S(1)} %compare_and_fusion.2, bf16[4,2,16,64,128]{4,3,2,1,0:T(8,128)(2,1)} %get-tuple-element.380, ...), kind=kOutput, calls=%fused_computation.6.clone.1 | convolution fusion | flops 275120128 | bytes 7221252 | tf_op jit(solution)/shard_map/while/body/eval_jaxpr/ikgd,knjd->kginj/dot_general | solution.py:86
  73.9 1.3 fusion.83
  75.2 0.9 copy_dynamic-update-slice_fusion.2
  76.1 2.4 %fusion.85 = f32[2,16,64,128]{3,2,1,0:T(8,128)S(1)} fusion(f32[2,16,64,64,8]{3,2,4,1,0:T(8,128)S(1)} %fusion.78, f32[2,8,64]{2,1,0:T(8,128)S(1)} %bitcast.226, pred[2,64,16,64]{1,3,2,0:T(8,128)(4,1)S(1)} %compare_and_fusion.2, f32[64,2,8]{0,2,1:T(8,128)S(1)} %bitcast.218, bf16[1,64,2,8,128]{4,3,2,1,0:T(8,128)(2,1)S(1)} %get-tuple-element.332), kind=kOutput, calls=%fused_computation.17.clone.1 | convolution fusion | flops 273022976 | bytes 5644288 | tf_op jit(solution)/shard_map/while/body/eval_jaxpr/kginj,ikgd->knjd/dot_general | solution.py:99
  78.5 0.9 fusion.86
  79.5 1.5 fusion.87
  81.0 1.0 constant_dynamic-slice_fusion.10
  81.9 1.3 fusion.78
  83.2 1.1 constant_dynamic-slice_fusion.11
  86.1 0.7 fusion.80
  87.3 4.0 %fusion.82 = bf16[2,8,64,16,64]{2,4,1,3,0:T(8,128)(2,1)S(1)} fusion(f32[2,16,64,64,8]{3,2,4,1,0:T(8,128)S(1)} %fusion.78, f32[2,8,64]{2,1,0:T(8,128)S(1)} %bitcast.224, f32[2,8,64]{2,1,0:T(8,128)S(1)} %bitcast.225, pred[2,64,16,64]{1,3,2,0:T(8,128)(4,1)S(1)} %compare_and_fusion.2, bf16[4,2,16,64,128]{4,3,2,1,0:T(8,128)(2,1)} %get-tuple-element.380, ...), kind=kOutput, calls=%fused_computation.6.clone.1 | convolution fusion | flops 275120128 | bytes 7221252 | tf_op jit(solution)/shard_map/while/body/eval_jaxpr/ikgd,knjd->kginj/dot_general | solution.py:86
  91.4 1.3 fusion.83
  92.7 0.9 copy_dynamic-update-slice_fusion.2
  93.6 2.4 %fusion.85 = f32[2,16,64,128]{3,2,1,0:T(8,128)S(1)} fusion(f32[2,16,64,64,8]{3,2,4,1,0:T(8,128)S(1)} %fusion.78, f32[2,8,64]{2,1,0:T(8,128)S(1)} %bitcast.226, pred[2,64,16,64]{1,3,2,0:T(8,128)(4,1)S(1)} %compare_and_fusion.2, f32[64,2,8]{0,2,1:T(8,128)S(1)} %bitcast.218, bf16[1,64,2,8,128]{4,3,2,1,0:T(8,128)(2,1)S(1)} %get-tuple-element.332), kind=kOutput, calls=%fused_computation.17.clone.1 | convolution fusion | flops 273022976 | bytes 5644288 | tf_op jit(solution)/shard_map/while/body/eval_jaxpr/kginj,ikgd->knjd/dot_general | solution.py:99
  96.0 0.9 fusion.86
  96.9 1.5 fusion.87
  98.6 19.0 %scatter_fusion = f32[8,64,2,256]{3,1,2,0:T(8,128)S(1)} fusion(f32[8,64,2,256]{3,1,2,0:T(8,128)S(1)} %broadcast_in_dim.53, s32[128]{0:T(128)S(1)} %reshape.136, f32[128,64,256]{2,1,0:T(8,128)} %bitcast.211), kind=kCustom, calls=%fused_computation.2 | custom fusion | flops 2097152 | bytes 25166848 | tf_op jit(solution)/shard_map/scatter-add | solution.py:127
  117.7 0.9 copy.44
  118.8 13.6 %all-gather = bf16[64,256]{1,0:T(8,128)(2,1)S(1)} all-gather(bf16[16,256]{1,0:T(8,128)(2,1)S(1)} %bitcast.229), channel_id=2, replica_groups=mesh['seq'=2,'head'=4,'dp'=4] {'head'}, dimensions={0}, use_global_device_ids=true | all-gather | bytes 40960 | tf_op jit(solution)/shard_map/all_gather | solution.py:138
  132.4 1.0 fusion.42
  133.4 1.5 reduce-scatter.2.cloned.1.call-done
  134.9 1.0 slice_bitcast_fusion
  135.9 0.8 copy.46
  136.7 0.8 copy.47
  137.5 26.9 %all-gather.4.cloned.1.call-done = f32[512,1280]{1,0:T(8,128)} async-done(((f32[64,1280]{1,0:T(8,128)}), f32[512,1280]{1,0:T(8,128)}) %all-gather.4.cloned.1.call-update) | async-done | bytes 2621456 | tf_op jit(solution)/shard_map/all_gather | solution.py:141
  164.4 1.9 %reduce_sum.27 = f32[64,1280]{1,0:T(8,128)S(1)} reduce(f32[8,64,1280]{2,1,0:T(8,128)} %bitcast.212, f32[]{:T(128)} %constant.29.clone.1), dimensions={0}, to_apply=%region_6.7 | reduce | flops 573440 | bytes 2949124 | tf_op jit(solution)/shard_map/reduce_sum | solution.py:141
  166.3 0.8 broadcast_multiply_fusion
  (50 shorter events, 5.7 us)
Async XLA Ops:
  8.0 124.4 %copy-start = (bf16[1,256,1280]{2,1,0:T(8,128)(2,1)S(1)}, bf16[1,256,1280]{2,1,0:T(8,128)(2,1)}, u32[]{:S(2)}) copy-start(bf16[1,256,1280]{2,1,0:T(8,128)(2,1)} %param.19) | copy-start | bytes 1966084
  8.0 20.5 %copy-start.1 = (f32[1,16,256]{2,1,0:T(8,128)S(1)}, f32[1,16,256]{2,1,0:T(8,128)}, u32[]{:S(2)}) copy-start(f32[1,16,256]{2,1,0:T(8,128)} %param.17) | copy-start | bytes 49156
  8.0 126.9 %reduce-scatter.2.cloned.1.call-start = ((), (), s32[]{:S(2)}) async-start(), calls=%async_computation.1 | async-start | bytes 786432 | tf_op jit(solution)/shard_map/reduce_scatter | solution.py:128
  118.6 45.8 %all-gather.4.cloned.1.call-start = ((), (), s32[]{:S(2)}) async-start(), calls=%async_computation.2 | async-start | bytes 2949120 | tf_op jit(solution)/shard_map/all_gather | solution.py:141
Sparse Core Ops, SparseCore 0:
  118.7 16.1 reduce-scatter.1
Sparse Core Ops, SparseCore 1:
  133.4 30.9 all-gather.3
